TPU v7x, 32 devices: a whole 2x2x4 slice. The times are simulated.
32 devices in a mesh: grp: 4 (over y, core), head: 8 (over z, x).
Axes of the slice: x: 2, y: 2, z: 4, core: 2. Of those that a mesh axis runs over, the one named last changes fastest.
Arguments:
- hidden_in: bfloat16 [96, 4096], P('grp', 'head'), may hold values from -6 to 6
- attention_gain: float32 [4096], replicated, may hold values from 0.1 to 1.9
- w_query: bfloat16 [4096, 4096], P(None, 'head'), may hold values from -0.09375 to 0.09375
- w_key_value: bfloat16 [2, 4096, 4096], P(None, None, 'head'), as said below
- w_attention_out: bfloat16 [4096, 4096], P('head'), may hold values from -0.09375 to 0.09375
- past_cache: bfloat16 [2, 96, 32, 128, 128], P(None, 'grp', 'head'), may hold values from -2000 to 2000, as said below
- lengths: int32 [96], P('grp'), may hold values from 2 to 128, as said below
- mamba_gain: float32 [4096], replicated, may hold values from 0.1 to 1.9
- w_in: bfloat16 [2, 4096, 8192], P(None, None, 'head'), may hold values from -0.09375 to 0.09375
- filter_weight: float32 [4, 8192], P(None, 'head'), may hold values from -3 to 3
- filter_bias: float32 [8192], P('head'), may hold values from -1.8 to 1.8
- filter_state: float32 [96, 3, 8192], P('grp', None, 'head'), may hold values from -6 to 6
- w_select: bfloat16 [8192, 288], P('head'), may hold values from -0.0625 to 0.0625
- w_step: bfloat16 [256, 8192], P(None, 'head'), may hold values from -0.375 to 0.375
- step_bias: float32 [8192], P('head'), may hold values from -4 to -1
- log_rate: float32 [16, 8192], P(None, 'head'), may hold values from 0 to 2.77
- skip_gain: float32 [8192], P('head'), may hold values from 0.1 to 1.9
- scan_state: float32 [96, 16, 8192], P('grp', None, 'head'), may hold values from -6 to 6
- w_mamba_out: bfloat16 [8192, 4096], P('head'), may hold values from -0.0625 to 0.0625
- reward_terms: float32 [96, 128], P('grp', 'head'), may hold values from -60 to 60
- reward_mask: int32 [96, 128], P('grp', 'head'), may hold values 0 or 1
Outputs:
- hidden_out: bfloat16 [96, 4096], P('grp', 'head')
- new_key_value: bfloat16 [2, 96, 32, 128], P(None, 'grp', 'head')
- new_filter_state: float32 [96, 3, 8192], P('grp', None, 'head')
- new_scan_state: float32 [96, 16, 8192], P('grp', None, 'head')
- rewards: float32 [96], P('grp')
Inputs may be any that keep to these rules, and one draw needn't show every extreme that they name: `w_key_value`: query heads that share a key-value head (4 of them in a row) hold equal copies. `past_cache`: query heads that share a key-value head (4 of them in a row) hold equal copies. `lengths`: the first sample's cache is full (128).
All inputs are finite; a program needn't handle non-finite values. No bound on the sum of `reward_mask` on one device may be relied on, other than what follows from the above.
Results may differ from a plain program's by a relative error of at most 0.012.
Values may be sent and summed in bfloat16 or wider, within the bound.
A program may use at most 128 MiB of HBM per device.

v0:
```python
import math

import jax
import jax.numpy as jnp
from jax import lax
from jax.sharding import PartitionSpec as P

EPS = 1e-06


def norm_rows(row_values, gain):
    values = row_values.astype(jnp.float32)
    factor = lax.rsqrt(jnp.mean(values * values, axis=-1, keepdims=True) + EPS)
    return (values * factor * gain).astype(jnp.bfloat16)


def attend_block(queries, past_cache, fresh, lengths):
    inv_root = 1.0 / math.sqrt(queries.shape[-1])
    scores = (
        jnp.einsum("bhd,bhtd->bht", queries, past_cache[0], preferred_element_type=jnp.float32)
        * inv_root
    )
    positions = lax.iota(jnp.int32, past_cache.shape[3])
    scores = jnp.where(positions[None, None, :] < lengths[:, None, None], scores, -jnp.inf)
    own_score = (
        jnp.einsum("bhd,bhd->bh", queries, fresh[0], preferred_element_type=jnp.float32) * inv_root
    )
    row_max = jnp.maximum(jnp.max(scores, axis=-1), own_score)
    weights = jnp.exp(scores - row_max[:, :, None])
    own_weight = jnp.exp(own_score - row_max)
    denominator = jnp.sum(weights, axis=-1) + own_weight
    weights = (weights / denominator[:, :, None]).astype(jnp.bfloat16)
    own_weight = (own_weight / denominator).astype(jnp.bfloat16)
    blended = jnp.einsum(
        "bht,bhtd->bhd", weights, past_cache[1], preferred_element_type=jnp.float32
    )
    blended = blended + own_weight.astype(jnp.float32)[:, :, None] * fresh[1].astype(jnp.float32)
    return blended.astype(jnp.bfloat16)


def reward_partial(reward_terms, reward_mask, lengths):
    columns = reward_terms.shape[1]
    positions = lax.axis_index("head") * columns + lax.iota(jnp.int32, columns)
    live = (reward_mask == 1) & (positions[None, :] < lengths[:, None])
    return jnp.sum(jnp.where(live, reward_terms, 0.0), axis=1)


def local(
    hidden_in,
    attention_gain,
    w_query,
    w_key_value,
    w_attention_out,
    past_cache,
    lengths,
    mamba_gain,
    w_in,
    filter_weight,
    filter_bias,
    filter_state,
    w_select,
    w_step,
    step_bias,
    log_rate,
    skip_gain,
    scan_state,
    w_mamba_out,
    reward_terms,
    reward_mask,
):
    samples = hidden_in.shape[0]
    shard_width = hidden_in.shape[1]
    local_heads = past_cache.shape[2]
    head_size = past_cache.shape[4]
    rank_width = w_step.shape[0]
    state_width = log_rate.shape[0]
    rewards = lax.psum(reward_partial(reward_terms, reward_mask, lengths), "head")
    full_in = lax.all_gather(hidden_in, "head", axis=1, tiled=True)
    normed = norm_rows(full_in, attention_gain)
    queries = jnp.dot(normed, w_query, preferred_element_type=jnp.float32).astype(jnp.bfloat16)
    queries = queries.reshape(samples, local_heads, head_size)
    fresh_all = jnp.einsum("bd,kdc->kbc", normed, w_key_value, preferred_element_type=jnp.float32)
    new_key_value = fresh_all.astype(jnp.bfloat16).reshape(2, samples, local_heads, head_size)
    attended = attend_block(queries, past_cache, new_key_value, lengths)
    attended = attended.reshape(samples, local_heads * head_size)
    head_terms = jnp.dot(attended, w_attention_out, preferred_element_type=jnp.float32)
    summed = lax.psum(head_terms, "head")
    mixed_full = (full_in.astype(jnp.float32) + summed).astype(jnp.bfloat16)
    mixed = lax.dynamic_slice_in_dim(
        mixed_full, lax.axis_index("head") * shard_width, shard_width, 1
    )
    normed_two = norm_rows(mixed_full, mamba_gain)
    x_inner = jnp.dot(normed_two, w_in[0], preferred_element_type=jnp.float32)
    gate_part = jnp.dot(normed_two, w_in[1], preferred_element_type=jnp.float32)
    taps = filter_weight.shape[0]
    conv_sum = filter_bias + x_inner * filter_weight[taps - 1]
    for tap_index in range(taps - 1):
        conv_sum = conv_sum + filter_state[:, tap_index, :] * filter_weight[tap_index]
    conv_out = jax.nn.silu(conv_sum).astype(jnp.bfloat16)
    new_filter_state = jnp.concatenate([filter_state[:, 1:, :], x_inner[:, None, :]], axis=1)
    local_select = jnp.dot(conv_out, w_select, preferred_element_type=jnp.float32)
    projected = lax.psum(local_select, "head")
    step_low = projected[:, :rank_width].astype(jnp.bfloat16)
    b_input = projected[:, rank_width : rank_width + state_width]
    c_output = projected[:, rank_width + state_width :]
    step_size = jax.nn.softplus(
        jnp.dot(step_low, w_step, preferred_element_type=jnp.float32) + step_bias
    )
    conv_value = conv_out.astype(jnp.float32)
    decay_rate = jnp.exp(-step_size[:, None, :] * jnp.exp(log_rate)[None, :, :])
    new_scan_state = (
        decay_rate * scan_state
        + step_size[:, None, :] * b_input[:, :, None] * conv_value[:, None, :]
    )
    scan_out = (
        jnp.sum(c_output[:, :, None] * new_scan_state, axis=1) + skip_gain * conv_value
    ) * jax.nn.silu(gate_part)
    scan_out = scan_out.astype(jnp.bfloat16)
    channel_terms = jnp.dot(scan_out, w_mamba_out, preferred_element_type=jnp.float32)
    mamba_sum = lax.psum_scatter(channel_terms, "head", scatter_dimension=1, tiled=True)
    hidden_out = (mixed.astype(jnp.float32) + mamba_sum).astype(jnp.bfloat16)
    return (hidden_out, new_key_value, new_filter_state, new_scan_state, rewards)


def solution(mesh):
    placed = (
        P("grp", "head"),
        P(),
        P(None, "head"),
        P(None, None, "head"),
        P("head", None),
        P(None, "grp", "head", None, None),
        P("grp"),
        P(),
        P(None, None, "head"),
        P(None, "head"),
        P("head"),
        P("grp", None, "head"),
        P("head", None),
        P(None, "head"),
        P("head"),
        P(None, "head"),
        P("head"),
        P("grp", None, "head"),
        P("head", None),
        P("grp", "head"),
        P("grp", "head"),
    )
    return jax.shard_map(
        local,
        mesh=mesh,
        in_specs=placed,
        out_specs=(
            P("grp", "head"),
            P(None, "grp", "head", None),
            P("grp", None, "head"),
            P("grp", None, "head"),
            P("grp"),
        ),
        check_vma=False,
    )
```

profile of v0, /device:TPU:0, one launch (start us, length us, event | category | flops | bytes accessed | tf_op | source)
XLA Modules:
  0.0 255.5 jit_solution(5977101583924743962)
XLA Ops:
  7.2 0.0 copy-start
  7.2 0.0 copy-start.4
  7.2 0.0 all-reduce.3.cloned.1.call-start
  7.2 32.8 %all_gather.3 = bf16[24,4096]{1,0:T(8,128)(2,1)S(1)} all-gather(bf16[24,512]{1,0:T(8,128)(2,1)} %param.21), channel_id=1, replica_groups=mesh['grp'=4,'head'=8] {'head'}, dimensions={1}, use_global_device_ids=true | all-gather | bytes 221184 | tf_op jit(solution)/shard_map/all_gather | solution.py:78
  40.0 0.2 fusion.16
  40.2 2.9 %convolution_convert_fusion.1 = bf16[24,512]{1,0:T(8,128)(2,1)S(1)} fusion(bf16[4096,512]{1,0:T(8,128)(2,1)} %param.23, bf16[24,4096]{1,0:T(8,128)(2,1)S(1)} %all_gather.3, f32[4096]{0:T(1024)} %param.22, f32[24]{0:T(128)S(1)} %add_rsqrt_fusion.1), kind=kOutput, calls=%fused_computation.17 | convolution fusion | flops 101068800 | bytes 4431968 | tf_op jit(solution)/shard_map/dot_general | solution.py:80
  43.2 0.0 copy-start.12
  43.2 4.6 %fusion.12 = bf16[2,24,512]{2,1,0:T(8,128)(2,1)S(1)} fusion(bf16[2,4096,512]{2,1,0:T(8,128)(2,1)} %param.24, bf16[24,4096]{1,0:T(8,128)(2,1)S(1)} %all_gather.3, f32[4096]{0:T(1024)S(1)} %copy-done.4, f32[24]{0:T(128)S(1)} %add_rsqrt_fusion.1), kind=kOutput, calls=%fused_computation.16 | convolution fusion | flops 201744384 | bytes 8650848 | tf_op jit(solution)/shard_map/bd,kdc->kbc/dot_general | solution.py:82
  47.9 0.1 fusion.31
  48.0 0.1 copy.32
  48.0 0.0 copy-done.12
  48.1 0.1 iota_compare_fusion
  48.1 3.6 %fusion.8 = f32[24,4,1,128]{3,2,1,0:T(1,128)S(1)} fusion(bf16[24,4,128,1]{2,3,1,0:T(2,128)(2,1)S(1)} %reshape.94, bf16[2,24,4,128,128]{4,3,2,1,0:T(8,128)(2,1)} %param.26), kind=kOutput, calls=%fused_computation.8 | convolution fusion | flops 3145728 | bytes 3219456 | tf_op jit(solution)/shard_map/bhd,bhtd->bht/dot_general | solution.py:20
  51.8 0.1 fusion.42
  51.8 0.2 fusion.41
  52.0 0.1 fusion.47
  52.2 0.0 copy-start.5
  52.2 0.0 copy-start.8
  52.2 0.0 copy-start.9
  52.2 0.0 copy-start.6
  52.2 0.0 copy-start.2
  52.2 0.0 copy-start.7
  52.2 0.0 copy-start.13
  52.2 2.9 %fusion.6 = f32[24,4,1,128]{3,2,1,0:T(1,128)S(1)} fusion(bf16[2,24,4,128,128]{4,3,2,1,0:T(8,128)(2,1)} %param.26, bf16[24,4,128,1]{2,0,1,3:T(8,128)(2,1)S(1)} %fusion.47), kind=kOutput, calls=%fused_computation.6 | convolution fusion | flops 3145728 | bytes 3219456 | tf_op jit(solution)/shard_map/bht,bhtd->bhd/dot_general | solution.py:34
  55.1 0.1 copy.26
  55.2 0.1 add_convert_fusion.1
  55.3 3.6 %fusion.43 = f32[24,4096]{1,0:T(8,128)} fusion(bf16[512,4096]{1,0:T(8,128)(2,1)} %param.25, bf16[3,8,4,128]{3,2,1,0:T(4,128)(2,1)S(1)} %bitcast.81), kind=kOutput, calls=%fused_computation.57 | convolution fusion | flops 100663296 | bytes 4612096 | tf_op jit(solution)/shard_map/dot_general | solution.py:86
  58.9 0.0 all-reduce.3.cloned.1.call-update
  58.9 0.0 reduce-scatter.2.cloned.1.call-start
  59.0 0.0 copy-done.5
  59.1 0.1 select_reduce_fusion
  59.2 72.6 %all-reduce.3.cloned.1.call-done = f32[24,4096]{1,0:T(8,128)} async-done(((f32[24,4096]{1,0:T(8,128)}), f32[24,4096]{1,0:T(8,128)}) %all-reduce.3.cloned.1.call-update) | async-done | bytes 393232 | tf_op jit(solution)/shard_map/psum | solution.py:87
  131.8 1.2 fusion.13
  133.0 0.0 copy-start.3
  133.0 0.0 copy-start.10
  133.0 0.0 copy-start.1
  133.1 5.5 %fusion.51 = (f32[24,1024]{1,0:T(8,128)}, bf16[24,1024]{1,0:T(8,128)(2,1)S(1)}, f32[24,1024]{1,0:T(8,128)S(1)}) fusion(f32[1024]{0:T(1024)S(1)} %bitcast.86, f32[24,3,1024]{2,0,1:T(8,128)S(1)} %copy-done.2, f32[1024]{0:T(1024)S(1)} %bitcast.87, f32[1024]{0:T(1024)S(1)} %bitcast.85, f32[1024]{0:T(1024)S(1)} %bitcast.84, f32[1024]{0:T(1024)S(1)} %copy-done.13, ...), kind=kOutput, calls=%fused_computation.75 | convolution fusion | flops 202063872 | bytes 9162848 | tf_op jit(solution)/shard_map/dot_general | solution.py:93
  138.5 0.3 fusion.56
  138.8 36.1 %all-reduce = (f32[24,288]{1,0:T(8,128)S(1)}, f32[24]{0:T(128)}) all-reduce(f32[24,288]{1,0:T(8,128)S(1)} %fusion.56, f32[24]{0:T(128)S(1)} %select_reduce_fusion), channel_id=1, replica_groups=mesh['grp'=4,'head'=8] {'head'}, use_global_device_ids=true, to_apply=%region_5.6 | all-reduce | flops 6936 | bytes 55488 | tf_op jit(solution)/shard_map/psum | solution.py:102
  174.9 0.1 fusion.53
  175.0 0.2 fusion.55
  175.2 2.8 %multiply_reduce_fusion = (f32[24,1024]{1,0:T(8,128)S(1)}, f32[24,16,1024]{2,1,0:T(8,128)}) fusion(f32[24,16]{1,0:T(8,128)S(1)} %get-tuple-element.16, f32[24,1024]{1,0:T(8,128)} %get-tuple-element.9, f32[24,16]{1,0:T(8,128)S(1)} %get-tuple-element.15, f32[24,1024]{1,0:T(8,128)S(1)} %get-tuple-element.25, f32[24,16,1024]{2,1,0:T(8,128)S(1)} %copy-done.1, ...), kind=kLoop, calls=%fused_computation.12 | loop fusion | flops 2727936 | bytes 3607552 | tf_op jit(solution)/shard_map/reduce_sum | solution.py:116
  178.1 8.9 %fusion.27 = f32[24,4096]{1,0:T(8,128)} fusion(bf16[1024,4096]{1,0:T(8,128)(2,1)} %param.39, bf16[2,4096,1024]{2,1,0:T(8,128)(2,1)} %param.29, f32[24,1024]{1,0:T(8,128)S(1)} %get-tuple-element.7, f32[1024]{0:T(1024)S(1)} %copy-done.11, bf16[24,4096]{1,0:T(8,128)(2,1)S(1)} %get-tuple-element.12, f32[4096]{0:T(1024)S(1)} %copy-done.7, ...), kind=kOutput, calls=%fused_computation.40 | convolution fusion | flops 403267584 | bytes 17535072 | tf_op jit(solution)/shard_map/dot_general | solution.py:119
  187.0 0.0 reduce-scatter.2.cloned.1.call-update
  187.0 0.6 reshape.84
  187.7 0.7 pad_maximum_fusion
  188.4 58.9 %reduce-scatter.2.cloned.1.call-done = f32[24,512]{1,0:T(8,128)} async-done(((f32[24,4096]{1,0:T(8,128)}), f32[24,512]{1,0:T(8,128)}) %reduce-scatter.2.cloned.1.call-update) | async-done | bytes 49168 | tf_op jit(solution)/shard_map/reduce_scatter | solution.py:120
  247.3 1.4 add_convert_fusion
  (27 shorter events, 0.2 us)
Async XLA Ops:
  7.2 131.4 %copy-start = (bf16[1024,288]{0,1:T(8,128)(2,1)S(1)}, bf16[1024,288]{0,1:T(8,128)(2,1)}, u32[]{:S(2)}) copy-start(bf16[1024,288]{0,1:T(8,128)(2,1)} %param.33) | copy-start | bytes 1769476
  7.2 36.0 %copy-start.4 = (f32[4096]{0:T(1024)S(1)}, f32[4096]{0:T(1024)}, u32[]{:S(2)}) copy-start(f32[4096]{0:T(1024)} %param.22) | copy-start | bytes 49156
  7.2 124.6 %all-reduce.3.cloned.1.call-start = ((), (), s32[]{:S(2)}) async-start(), calls=%async_computation.1 | async-start | bytes 786432 | tf_op jit(solution)/shard_map/psum | solution.py:87
  43.2 4.9 %copy-start.12 = (s32[24]{0:T(128)S(1)}, s32[24]{0:T(128)}, u32[]{:S(2)}) copy-start(s32[24]{0:T(128)} %param.27) | copy-start | bytes 292
  52.2 6.8 %copy-start.5 = (f32[16,1024]{1,0:T(8,128)S(1)}, f32[16,1024]{1,0:T(8,128)}, u32[]{:S(2)}) copy-start(f32[16,1024]{1,0:T(8,128)} %param.36) | copy-start | bytes 196612
  52.2 6.9 %copy-start.8 = (f32[24,16]{0,1:T(8,128)S(1)}, f32[24,16]{0,1:T(8,128)}, u32[]{:S(2)}) copy-start(f32[24,16]{0,1:T(8,128)} %param.40) | copy-start | bytes 4612
  52.2 6.9 %copy-start.9 = (s32[24,16]{0,1:T(8,128)S(1)}, s32[24,16]{0,1:T(8,128)}, u32[]{:S(2)}) copy-start(s32[24,16]{0,1:T(8,128)} %param.41) | copy-start | bytes 4612
  52.2 7.0 %copy-start.6 = (f32[4,1024]{1,0:T(4,128)S(1)}, f32[4,1024]{1,0:T(4,128)}, u32[]{:S(2)}) copy-start(f32[4,1024]{1,0:T(4,128)} %param.30) | copy-start | bytes 49156
  52.2 80.8 %copy-start.2 = (f32[24,3,1024]{2,0,1:T(8,128)S(1)}, f32[24,3,1024]{2,0,1:T(8,128)}, u32[]{:S(2)}) copy-start(f32[24,3,1024]{2,0,1:T(8,128)} %param.32) | copy-start | bytes 884740
  52.2 80.8 %copy-start.7 = (f32[4096]{0:T(1024)S(1)}, f32[4096]{0:T(1024)}, u32[]{:S(2)}) copy-start(f32[4096]{0:T(1024)} %param.28) | copy-start | bytes 49156
  52.2 80.8 %copy-start.13 = (f32[1024]{0:T(1024)S(1)}, f32[1024]{0:T(1024)}, u32[]{:S(2)}) copy-start(f32[1024]{0:T(1024)} %param.31) | copy-start | bytes 12292
  58.9 188.3 %reduce-scatter.2.cloned.1.call-start = ((), (), s32[]{:S(2)}) async-start(), calls=%async_computation.2 | async-start | bytes 442368 | tf_op jit(solution)/shard_map/reduce_scatter | solution.py:120
  133.0 41.9 %copy-start.3 = (bf16[256,1024]{1,0:T(8,128)(2,1)S(1)}, bf16[256,1024]{1,0:T(8,128)(2,1)}, u32[]{:S(2)}) copy-start(bf16[256,1024]{1,0:T(8,128)(2,1)} %param.34) | copy-start | bytes 1572868
  133.0 41.9 %copy-start.10 = (f32[1024]{0:T(1024)S(1)}, f32[1024]{0:T(1024)}, u32[]{:S(2)}) copy-start(f32[1024]{0:T(1024)} %param.35) | copy-start | bytes 12292
  133.0 42.2 %copy-start.1 = (f32[24,16,1024]{2,1,0:T(8,128)S(1)}, f32[24,16,1024]{2,1,0:T(8,128)}, u32[]{:S(2)}) copy-start(f32[24,16,1024]{2,1,0:T(8,128)} %param.38) | copy-start | bytes 4718596
  138.5 39.5 %copy-start.11 = (f32[1024]{0:T(1024)S(1)}, f32[1024]{0:T(1024)}, u32[]{:S(2)}) copy-start(f32[1024]{0:T(1024)} %param.37) | copy-start | bytes 12292
  178.1 9.6 %slice-start = ((f32[24,3,1024]{2,0,1:T(8,128)}), f32[24,2,1024]{2,0,1:T(8,128)S(1)}, s32[]{:S(2)}) async-start(f32[24,3,1024]{2,0,1:T(8,128)} %param.32), calls=%async_computation.3 | async-start | bytes 393216 | tf_op jit(solution)/shard_map/slice | solution.py:100
Sparse Core Ops, SparseCore 0:
  59.1 72.7 all-reduce.2
  187.2 60.0 reduce-scatter.1
where the time goes:
time: 256 us
  waiting for transfers between devices  132 us (52%)
  blocking collectives  68.9 us (27%)
  matrix products  32.5 us (13%)
  between operations  14.3 us (6%)
  other arithmetic  7.1 us (3%)
    psum x1, waiting for transfers between devices, local(): summed = lax.psum(head_terms, 'head')  72.6 us
    reduce_scatter x1, waiting for transfers between devices, local(): lax.psum_scatter(channel_terms, 'head', scatter_dimension=1, tiled=True)  58.9 us
    psum x1, blocking collectives, local(): projected = lax.psum(local_select, 'head')  36.1 us
    all_gather x1, blocking collectives, local(): full_in = lax.all_gather(hidden_in, 'head', axis=1, tiled=True)  32.8 us
    dot_general x1, matrix products, local(): jnp.dot(scan_out, w_mamba_out, preferred_element_type=jnp.float32)  8.95 us
    dot_general x1, matrix products, local(): x_inner = jnp.dot(normed_two, w_in[0], preferred_element_type=jnp.float32)  5.46 us
  transfers between devices with their start and end apart: 2, of which 2 were waited for; matrix products, arithmetic and copies ran while one was open for 1% of the time, Pallas kernels for 0%

commit v1 on v0

v1 whole, which is shorter than its diff:
```python
import functools
import math

import jax
import jax.numpy as jnp
from jax import lax
from jax.experimental import pallas as pl
from jax.experimental.pallas import tpu as pltpu
from jax.sharding import PartitionSpec as P

EPS = 1e-06
SHARE = 4
LANES = 128
BF16 = jnp.bfloat16
F32 = jnp.float32
MESH = pl.DeviceIdType.MESH


def dot(a, b):
    return jnp.dot(a, b, preferred_element_type=F32)


def columns_of(index, width):
    return pl.ds(pl.multiple_of(index * width, width), width)


def tile_of(width):
    for tile in (512, 256):
        if width % tile == 0:
            return tile
    return width


def matmul(x_ref, w_ref, out_ref):
    width = w_ref.shape[1]
    tile = tile_of(width)

    def body(i, carry):
        cols = columns_of(i, tile)
        out_ref[:, cols] = dot(x_ref[...], w_ref[:, cols])
        return carry

    lax.fori_loop(0, width // tile, body, 0)


def norm_blocks(blocks, gain, out, width):
    n, samples = blocks.shape[0], blocks.shape[1]
    total = jnp.zeros((samples, 1), F32)
    for j in range(n):
        v = blocks[j].astype(F32)
        total = total + jnp.sum(v * v, axis=1, keepdims=True)
    factor = lax.rsqrt(total / (n * width) + EPS)
    for j in range(n):
        cols = slice(j * width, (j + 1) * width)
        out[:, cols] = (blocks[j].astype(F32) * factor * gain[:, cols]).astype(BF16)


def kernel(n, *refs):
    (
        hidden, again, wq, wkv, wao, cache, lengths, mgain, w_in, fw, fb, fs, wsel,
        wstep, sbias, lrate, skip, scan, wmo, rterm, rmask,
        hidden_out, nkv_out, nfs_out, scan_out, rew_out,
        full, v_again, v_wq, v_wkv, v_wao, v_cache, v_mgain, v_win, v_fw, v_fb, v_fs,
        v_wsel, v_wstep, v_sbias, v_lrate, v_skip, v_scan, v_wmo, v_rterm, v_rmask,
        normed, q3, kv3, len3, q2, kv2, send_a, recv_a, mixfull, xin, gate, nfs,
        sel_msg, conv, step, yrow, sout, send_b, recv_b, hout, bct, rew,
        load_sem, out_sem, send_sem, recv_sem,
    ) = refs
    me = lax.axis_index("head")
    samples, width = hidden.shape
    heads, head_size = cache.shape[2], cache.shape[4]
    groups = v_cache.shape[2]
    share = heads // groups
    rank = wstep.shape[0]
    states = lrate.shape[0]
    channels = lrate.shape[1]
    taps = fw.shape[0]

    loads = {}

    def load(name, src, dst, pieces=1):
        sem = load_sem.at[len(loads)]
        rows = src.shape[0]
        step_rows = rows // pieces
        for p in range(pieces):
            part = pl.ds(p * step_rows, step_rows)
            if pieces == 1:
                pltpu.make_async_copy(src, dst, sem).start()
            else:
                pltpu.make_async_copy(src.at[part], dst.at[part], sem).start()
        loads[name] = pltpu.make_async_copy(src, dst, sem)

    load("hidden", hidden, full.at[me])
    load("again", again, v_again)
    load("wq", wq, v_wq, 4)
    for g in range(groups):
        cols = pl.ds(g * share * head_size, head_size)
        mine = pl.ds(g * head_size, head_size)
        for i in range(2):
            load(("wkv", i, g), wkv.at[i, :, cols], v_wkv.at[i, :, mine], 2)
    for i in range(2):
        for g in range(groups):
            load(("cache", i, g), cache.at[i, :, g * share], v_cache.at[i, :, g])
    load("wao", wao, v_wao, 4)

    peers = [lax.rem(me + d, n) for d in range(1, n)]
    barrier = pltpu.get_barrier_semaphore()
    for peer in peers:
        pl.semaphore_signal(barrier, inc=1, device_id={"head": peer}, device_id_type=MESH)
    pl.semaphore_wait(barrier, n - 1)

    sent = []

    def send(stage, src, dst, d):
        copy = pltpu.make_async_remote_copy(
            src_ref=src,
            dst_ref=dst,
            send_sem=send_sem.at[stage, d],
            recv_sem=recv_sem.at[stage, me],
            device_id={"head": peers[d - 1]},
            device_id_type=MESH,
        )
        copy.start()
        sent.append(copy)

    def arrived(stage, dst_of, d):
        source = lax.rem(me + n - d, n)
        pltpu.make_async_remote_copy(
            src_ref=dst_of(source),
            dst_ref=dst_of(source),
            send_sem=send_sem.at[stage, d],
            recv_sem=recv_sem.at[stage, source],
            device_id={"head": peers[d - 1]},
            device_id_type=MESH,
        ).wait_recv()
        return source

    loads["hidden"].wait()
    for d in range(1, n):
        send(0, full.at[me], full.at[me], d)

    load("rterm", rterm, v_rterm)
    load("rmask", rmask, v_rmask)
    load("mgain", mgain, v_mgain)
    load("fw", fw, v_fw)
    load("fb", fb, v_fb)
    load("fs", fs, v_fs)
    load("win0", w_in.at[0], v_win.at[0], 8)
    load("wsel", wsel, v_wsel)
    load("win1", w_in.at[1], v_win.at[1], 8)
    load("wstep", wstep, v_wstep)
    load("sbias", sbias, v_sbias)
    load("lrate", lrate, v_lrate)
    load("skip", skip, v_skip)
    load("scan", scan, v_scan, 2 if samples % 2 == 0 else 1)
    load("wmo", wmo, v_wmo, 8)

    for b in range(samples):
        len3[b] = jnp.full((8, LANES), lengths[b], jnp.int32)
    loads["rterm"].wait()
    loads["rmask"].wait()
    cols_r = rterm.shape[1]
    len2 = len3[:, 0, :][:, :cols_r]
    place = me * cols_r + lax.broadcasted_iota(jnp.int32, (samples, cols_r), 1)
    live = (v_rmask[...] == 1) & (place < len2)
    part = jnp.sum(jnp.where(live, v_rterm[...], 0.0), axis=1, keepdims=True)
    high = part.astype(BF16).astype(F32)
    low = (part - high).astype(BF16).astype(F32)
    rest = part - high - low
    lane = lax.broadcasted_iota(jnp.int32, (samples, LANES), 1)
    pieces = jnp.where(lane == 0, high, jnp.where(lane == 1, low, jnp.where(lane == 2, rest, 0.0)))
    sel_msg[me] = jnp.zeros(sel_msg.shape[1:], BF16)
    sel_width = sel_msg.shape[2] - LANES
    sel_msg[me, :, sel_width:] = pieces.astype(BF16)

    loads["again"].wait()
    for d in range(1, n):
        arrived(0, lambda s: full.at[s], d)
    norm_blocks(full, v_again, normed, width)

    loads["wq"].wait()
    matmul(normed, v_wq, q2)
    for g in range(groups):
        for i in range(2):
            loads[("wkv", i, g)].wait()
    inv_root = 1.0 / math.sqrt(head_size)
    for i in range(2):
        fresh = dot(normed[...], v_wkv[i]).astype(BF16)
        for g in range(groups):
            one = fresh[:, g * head_size : (g + 1) * head_size]
            for s in range(share):
                h = g * share + s
                kv2[i, :, h * head_size : (h + 1) * head_size] = one
            wide = one.astype(F32)
            for s in range(8):
                kv3[i, g, :, s, :] = wide
    pltpu.make_async_copy(kv2, nkv_out, out_sem.at[0]).start()
    q3[...] = jnp.zeros_like(q3)
    for g in range(groups):
        for s in range(share):
            h = g * share + s
            q3[g, :, s, :] = q2[:, h * head_size : (h + 1) * head_size].astype(BF16).astype(F32)
    context = v_cache.shape[3]
    for g in range(groups):
        loads[("cache", 0, g)].wait()
        loads[("cache", 1, g)].wait()
        q = q3[g]
        scores = lax.dot_general(
            q.astype(BF16), v_cache[0, :, g], (((2,), (2,)), ((0,), (0,))),
            preferred_element_type=F32,
        ) * inv_root
        place3 = lax.broadcasted_iota(jnp.int32, (samples, 8, context), 2)
        scores = jnp.where(place3 < len3[...][:, :, :1], scores, -jnp.inf)
        own = jnp.sum(q * kv3[0, g], axis=2, keepdims=True) * inv_root
        top = jnp.maximum(jnp.max(scores, axis=2, keepdims=True), own)
        weights = jnp.exp(scores - top)
        own_w = jnp.exp(own - top)
        denom = jnp.sum(weights, axis=2, keepdims=True) + own_w
        weights = (weights / denom).astype(BF16)
        own_w = (own_w / denom).astype(BF16).astype(F32)
        blended = lax.dot_general(
            weights, v_cache[1, :, g], (((2,), (1,)), ((0,), (0,))),
            preferred_element_type=F32,
        )
        q3[g] = blended + own_w * kv3[1, g]
    attended = jnp.concatenate(
        [q3[g, :, s, :] for g in range(groups) for s in range(share)], axis=1
    ).astype(BF16)

    loads["wao"].wait()
    for d in range(1, n):
        send_a[d] = dot(attended, v_wao[:, columns_of(peers[d - 1], width)]).astype(BF16)
        send(1, send_a.at[d], recv_a.at[me], d)
    mixed = full[me].astype(F32) + dot(attended, v_wao[:, columns_of(me, width)])
    for d in range(1, n):
        source = arrived(1, lambda s: recv_a.at[s], d)
        mixed = mixed + recv_a[source].astype(F32)
    mixfull[me] = mixed.astype(BF16)
    for d in range(1, n):
        send(2, mixfull.at[me], mixfull.at[me], d)
    loads["mgain"].wait()
    loads["fw"].wait()
    loads["fb"].wait()
    loads["fs"].wait()
    loads["win0"].wait()
    loads["wsel"].wait()
    base = jnp.broadcast_to(v_fb[...], (samples, channels))
    for k in range(taps - 1):
        base = base + v_fs[:, k, :] * v_fw[k : k + 1, :]
    conv[...] = base
    for k in range(taps - 2):
        nfs[:, k, :] = v_fs[:, k + 1, :]
    for d in range(1, n):
        arrived(2, lambda s: mixfull.at[s], d)
    norm_blocks(mixfull, v_mgain, normed, width)

    matmul(normed, v_win.at[0], xin)
    x_inner = xin[...]
    conv_sum = conv[...] + x_inner * v_fw[taps - 1 : taps, :]
    conv_b = (conv_sum * jax.nn.sigmoid(conv_sum)).astype(BF16)
    conv[...] = conv_b.astype(F32)
    sel_msg[me, :, :rank] = dot(conv_b, v_wsel[:, :rank]).astype(BF16)
    sel_msg[me, :, rank : rank + 2 * states] = dot(conv_b, v_wsel[:, rank:]).astype(BF16)
    for d in range(1, n):
        send(3, sel_msg.at[me], sel_msg.at[me], d)
    nfs[:, taps - 2, :] = x_inner
    pltpu.make_async_copy(nfs, nfs_out, out_sem.at[1]).start()
    loads["win1"].wait()
    matmul(normed, v_win.at[1], gate)
    g_part = gate[...]
    gate[...] = g_part * jax.nn.sigmoid(g_part)
    for name in ("wstep", "sbias", "lrate", "skip", "scan"):
        loads[name].wait()
    rate = -jnp.exp(v_lrate[...])
    v_lrate[...] = rate
    for d in range(1, n):
        arrived(3, lambda s: sel_msg.at[s], d)
    projected = sel_msg[0].astype(F32)
    for j in range(1, n):
        projected = projected + sel_msg[j].astype(F32)
    step_low = projected[:, :rank].astype(BF16)
    raw = dot(step_low, v_wstep[...]) + v_sbias[...]
    step[...] = jnp.maximum(raw, 0.0) + jnp.log1p(jnp.exp(-jnp.abs(raw)))
    bct[...] = jnp.zeros_like(bct)
    bct[:samples, :] = projected[:, rank : rank + LANES]
    flipped = jnp.transpose(bct[...])
    bct[...] = flipped
    total = jnp.sum(projected[:, sel_width:], axis=1, keepdims=True)
    diagonal = lax.broadcasted_iota(jnp.int32, (samples, LANES), 0) == lane
    row = jnp.sum(jnp.where(diagonal, total, 0.0), axis=0, keepdims=True)
    rew[...] = row[:, :samples]

    for b in range(samples):
        now = step[b : b + 1, :]
        decay = jnp.exp(now * v_lrate[...])
        b_col = bct[:states, b : b + 1]
        c_col = bct[states : 2 * states, b : b + 1]
        state = decay * v_scan[b] + b_col * (now * conv[b : b + 1, :])
        v_scan[b] = state
        yrow[b : b + 1, :] = jnp.sum(c_col * state, axis=0, keepdims=True)
    pltpu.make_async_copy(v_scan, scan_out, out_sem.at[2]).start()
    sout[...] = ((yrow[...] + v_skip[...] * conv[...]) * gate[...]).astype(BF16)

    loads["wmo"].wait()
    for d in range(1, n):
        send_b[d] = dot(sout[...], v_wmo[:, columns_of(peers[d - 1], width)]).astype(BF16)
        send(4, send_b.at[d], recv_b.at[me], d)
    final = mixfull[me].astype(F32) + dot(sout[...], v_wmo[:, columns_of(me, width)])
    pltpu.make_async_copy(rew, rew_out, out_sem.at[3]).start()
    for d in range(1, n):
        source = arrived(4, lambda s: recv_b.at[s], d)
        final = final + recv_b[source].astype(F32)
    hout[...] = final.astype(BF16)
    pltpu.make_async_copy(hout, hidden_out, out_sem.at[4]).start()
    for copy in sent:
        copy.wait_send()
    for i, (src, dst) in enumerate(
        ((kv2, nkv_out), (nfs, nfs_out), (v_scan, scan_out), (rew, rew_out), (hout, hidden_out))
    ):
        pltpu.make_async_copy(src, dst, out_sem.at[i]).wait()


def local(n, *args):
    (
        hidden, again, wq, wkv, wao, cache, lengths, mgain, w_in, fw, fb, fs, wsel,
        wstep, sbias, lrate, skip, scan, wmo, rterm, rmask,
    ) = args
    samples, width = hidden.shape
    heads, context, head_size = cache.shape[2:]
    share = min(SHARE, heads)
    groups = heads // share
    model = wq.shape[0]
    states, channels = lrate.shape
    row = lambda a: a.reshape(1, a.shape[0])
    args = (
        hidden, row(again), wq, wkv, wao, cache, lengths, row(mgain), w_in, fw, row(fb), fs,
        wsel, wstep, row(sbias), lrate, row(skip), scan, wmo, rterm, rmask,
    )
    sel_pad = -(-wsel.shape[1] // LANES) * LANES + LANES
    same = lambda a: pltpu.VMEM(a.shape, a.dtype)
    scratch = [
        pltpu.VMEM((n, samples, width), BF16),
        same(args[1]),
        same(wq),
        pltpu.VMEM((2, model, groups * head_size), BF16),
        same(wao),
        pltpu.VMEM((2, samples, groups, context, head_size), BF16),
        same(args[7]),
        same(w_in),
        same(fw),
        same(args[10]),
        same(fs),
        same(wsel),
        same(wstep),
        same(args[14]),
        same(lrate),
        same(args[16]),
        same(scan),
        same(wmo),
        same(rterm),
        same(rmask),
        pltpu.VMEM((samples, model), BF16),
        pltpu.VMEM((groups, samples, 8, head_size), F32),
        pltpu.VMEM((2, groups, samples, 8, head_size), F32),
        pltpu.VMEM((samples, 8, LANES), jnp.int32),
        pltpu.VMEM((samples, heads * head_size), F32),
        pltpu.VMEM((2, samples, heads * head_size), BF16),
        pltpu.VMEM((n, samples, width), BF16),
        pltpu.VMEM((n, samples, width), BF16),
        pltpu.VMEM((n, samples, width), BF16),
        pltpu.VMEM((samples, channels), F32),
        pltpu.VMEM((samples, channels), F32),
        same(fs),
        pltpu.VMEM((n, samples, sel_pad), BF16),
        pltpu.VMEM((samples, channels), F32),
        pltpu.VMEM((samples, channels), F32),
        pltpu.VMEM((samples, channels), F32),
        pltpu.VMEM((samples, channels), BF16),
        pltpu.VMEM((n, samples, width), BF16),
        pltpu.VMEM((n, samples, width), BF16),
        pltpu.VMEM((samples, width), BF16),
        pltpu.VMEM((LANES, LANES), F32),
        pltpu.VMEM((1, samples), F32),
        pltpu.SemaphoreType.DMA((19 + 4 * groups,)),
        pltpu.SemaphoreType.DMA((5,)),
        pltpu.SemaphoreType.DMA((5, n)),
        pltpu.SemaphoreType.DMA((5, n)),
    ]
    in_specs = [pl.BlockSpec(memory_space=pl.ANY)] * len(args)
    in_specs[6] = pl.BlockSpec(memory_space=pltpu.SMEM)
    hidden_out, nkv, nfs, new_scan, rewards = pl.pallas_call(
        functools.partial(kernel, n),
        out_shape=(
            jax.ShapeDtypeStruct((samples, width), BF16),
            jax.ShapeDtypeStruct((2, samples, heads * head_size), BF16),
            jax.ShapeDtypeStruct(fs.shape, F32),
            jax.ShapeDtypeStruct(scan.shape, F32),
            jax.ShapeDtypeStruct((1, samples), F32),
        ),
        in_specs=in_specs,
        out_specs=[pl.BlockSpec(memory_space=pl.ANY)] * 5,
        scratch_shapes=scratch,
        compiler_params=pltpu.CompilerParams(
            collective_id=0, has_side_effects=True, vmem_limit_bytes=67043328
        ),
        name="decode_step",
    )(*args)
    return (
        hidden_out,
        nkv.reshape(2, samples, heads, head_size),
        nfs,
        new_scan,
        rewards.reshape(samples),
    )


def solution(mesh):
    placed = (
        P("grp", "head"),
        P(),
        P(None, "head"),
        P(None, None, "head"),
        P("head", None),
        P(None, "grp", "head", None, None),
        P("grp"),
        P(),
        P(None, None, "head"),
        P(None, "head"),
        P("head"),
        P("grp", None, "head"),
        P("head", None),
        P(None, "head"),
        P("head"),
        P(None, "head"),
        P("head"),
        P("grp", None, "head"),
        P("head", None),
        P("grp", "head"),
        P("grp", "head"),
    )
    return jax.shard_map(
        functools.partial(local, mesh.shape["head"]),
        mesh=mesh,
        in_specs=placed,
        out_specs=(
            P("grp", "head"),
            P(None, "grp", "head", None),
            P("grp", None, "head"),
            P("grp", None, "head"),
            P("grp"),
        ),
        check_vma=False,
    )
```

time: 256 us -> 58 us (0.23)
  waiting for transfers between devices: 132 us -> 0 us
  blocking collectives: 68.9 us -> 0 us
  Pallas kernels: 0 us -> 41.5 us
  matrix products: 32.5 us -> 0 us
  local copies, waits for them, and re-layouts: 1.08 us -> 15.4 us
  between operations: 14.3 us -> 0.64 us
  other arithmetic: 7.1 us -> 0 us
    psum x1 -> x0, waiting for transfers between devices: 72.6 us -> none  [local(): summed = lax.psum(head_terms, 'head')]
    reduce_scatter x1 -> x0, waiting for transfers between devices: 58.9 us -> none  [local(): lax.psum_scatter(channel_terms, 'head', scatter_dimension=1, tiled=True)]
    pallas_call x0 -> x1, Pallas kernels: none -> 41.5 us  [local(): pl.pallas_call(functools.partial(kernel, n), out_shape=(jax.ShapeDtypeStr...]
    psum x1 -> x0, blocking collectives: 36.1 us -> none  [local(): projected = lax.psum(local_select, 'head')]
    all_gather x1 -> x0, blocking collectives: 32.8 us -> none  [local(): full_in = lax.all_gather(hidden_in, 'head', axis=1, tiled=True)]
    dot_general x9 -> x0, matrix products: 32.5 us -> none  [the longest x1 8.95 us: local(): jnp.dot(scan_out, w_mamba_out, preferred_element_type=jnp.float32)]
    unnamed x28 -> x8, local copies, waits for them, and re-layouts: 0.09 us -> 14 us
    reduce_sum x5 -> x0, other arithmetic: 4.44 us -> none  [the longest x1 2.85 us: local(): jnp.sum(c_output[:, :, None] * new_scan_state, axis=1)]
  transfers between devices with their start and end apart: 2 -> 0, of which waited for: 2 -> 0; matrix products, arithmetic and copies ran while one was open for 1% -> 0% of each run, Pallas kernels for 0% -> 0%
where the time goes in v1:
time: 58 us; the launch traced here: 57.5 us
  Pallas kernels  41.5 us (72%)
  local copies, waits for them, and re-layouts  15.4 us (27%)
  between operations  0.64 us (1%)
    pallas_call x1, Pallas kernels, local(): pl.pallas_call(functools.partial(kernel, n), out_shape=(jax.ShapeDtypeStr...  41.5 us
    unnamed x8, local copies, waits for them, and re-layouts  14 us
    reshape x1, local copies, waits for them, and re-layouts, local(): nkv.reshape(2, samples, heads, head_size)  1.44 us

profile of v1, /device:TPU:0, one launch (start us, length us, event | category | flops | bytes accessed | tf_op | source)
XLA Modules:
  0.0 57.5 jit_solution(8102307162791403428)
XLA Ops:
  0.6 1.4 %copy.28.refs_19_ = f32[24,16]{1,0:T(8,128)} copy(f32[24,16]{0,1:T(8,128)} %param.40) | data formatting | bytes 3072 | tf_op args[19]
  2.0 1.4 %copy.29.refs_20_ = s32[24,16]{1,0:T(8,128)} copy(s32[24,16]{0,1:T(8,128)} %param.41) | data formatting | bytes 3072 | tf_op args[20]
  3.4 1.9 %copy.26.refs_11_ = f32[24,3,1024]{2,1,0:T(4,128)} copy(f32[24,3,1024]{2,0,1:T(8,128)} %param.32) | data formatting | bytes 589824 | tf_op args[11]
  5.3 2.2 %copy.27.refs_12_ = bf16[1024,288]{1,0:T(8,128)(2,1)} copy(bf16[1024,288]{0,1:T(8,128)(2,1)} %param.33) | data formatting | bytes 1179648 | tf_op args[12]
  7.5 41.5 %decode_step.1 = (bf16[24,512]{1,0:T(8,128)(2,1)}, bf16[2,24,512]{2,1,0:T(8,128)(2,1)}, f32[24,3,1024]{2,1,0:T(4,128)}, f32[24,16,1024]{2,1,0:T(8,128)}, f32[1,24]{1,0:T(1,128)}) custom-call(bf16[24,512]{1,0:T(8,128)(2,1)} %refs_0_.1, f32[1,4096]{1,0:T(1,128)} %bitcast.6, bf16[4096,512]{1,0:T(8,128)(2,1)} %refs_2_.1, bf16[2,4096,512]{2,1,0:T(8,128)(2,1)} %refs_3_.1, ...), custom_call_target="tpu_custom_call" | custom-call | tf_op jit(solution)/shard_map/decode_step/pallas_call | solution.py:391
  49.0 1.4 %reshape.36 = bf16[2,24,4,128]{3,2,1,0:T(4,128)(2,1)} reshape(bf16[2,24,512]{2,1,0:T(8,128)(2,1)} %get-tuple-element.11) | data formatting | bytes 98304 | tf_op jit(solution)/shard_map/reshape | solution.py:410
  50.4 1.9 %copy.30 = f32[24,3,1024]{2,0,1:T(8,128)} copy(f32[24,3,1024]{2,1,0:T(4,128)} %get-tuple-element.17) | data formatting | bytes 589824
  52.3 1.3 %copy.34 = bf16[24,512]{1,0:T(8,128)(2,1)} copy(bf16[24,512]{1,0:T(8,128)(2,1)} %get-tuple-element.25) | data formatting | bytes 49152
  53.6 2.7 %copy.35 = f32[24,16,1024]{2,1,0:T(8,128)} copy(f32[24,16,1024]{2,1,0:T(8,128)} %get-tuple-element.28) | data formatting | bytes 3145728
  56.3 1.2 %copy.36 = f32[24]{0:T(128)} copy(f32[24]{0:T(128)} %bitcast.11) | data formatting | bytes 192

commit v2 on v1

--- a/solution.py
+++ b/solution.py
@@ -63,7 +63,7 @@
         full, v_again, v_wq, v_wkv, v_wao, v_cache, v_mgain, v_win, v_fw, v_fb, v_fs,
         v_wsel, v_wstep, v_sbias, v_lrate, v_skip, v_scan, v_wmo, v_rterm, v_rmask,
         normed, q3, kv3, len3, q2, kv2, send_a, recv_a, mixfull, xin, gate, nfs,
-        sel_msg, conv, step, yrow, sout, send_b, recv_b, hout, bct, rew,
+        sel_msg, conv, step, yrow, sout, send_b, recv_b, hout, bct, rew, pieces,
         load_sem, out_sem, send_sem, recv_sem,
     ) = refs
     me = lax.axis_index("head")
@@ -146,7 +146,7 @@
     load("fb", fb, v_fb)
     load("fs", fs, v_fs)
     load("win0", w_in.at[0], v_win.at[0], 8)
-    load("wsel", wsel, v_wsel)
+    load("wsel", wsel, v_wsel.at[pl.ds(0, wsel.shape[0])])
     load("win1", w_in.at[1], v_win.at[1], 8)
     load("wstep", wstep, v_wstep)
     load("sbias", sbias, v_sbias)
@@ -159,19 +159,25 @@
         len3[b] = jnp.full((8, LANES), lengths[b], jnp.int32)
     loads["rterm"].wait()
     loads["rmask"].wait()
-    cols_r = rterm.shape[1]
-    len2 = len3[:, 0, :][:, :cols_r]
-    place = me * cols_r + lax.broadcasted_iota(jnp.int32, (samples, cols_r), 1)
-    live = (v_rmask[...] == 1) & (place < len2)
-    part = jnp.sum(jnp.where(live, v_rterm[...], 0.0), axis=1, keepdims=True)
+    count = rterm.shape[0]
+    diagonal = lax.broadcasted_iota(jnp.int32, (samples, samples), 0) == lax.broadcasted_iota(
+        jnp.int32, (samples, samples), 1
+    )
+    len_row = jnp.sum(jnp.where(diagonal, len3[:, 0, :][:, :samples], 0), axis=0, keepdims=True)
+    place = me * count + lax.broadcasted_iota(jnp.int32, (count, samples), 0)
+    live = (v_rmask[...] == 1) & (place < len_row)
+    part_row = jnp.sum(jnp.where(live, v_rterm[...], 0.0), axis=0, keepdims=True)
+    part = jnp.sum(jnp.where(diagonal, part_row, 0.0), axis=1, keepdims=True)
     high = part.astype(BF16).astype(F32)
     low = (part - high).astype(BF16).astype(F32)
     rest = part - high - low
-    lane = lax.broadcasted_iota(jnp.int32, (samples, LANES), 1)
-    pieces = jnp.where(lane == 0, high, jnp.where(lane == 1, low, jnp.where(lane == 2, rest, 0.0)))
-    sel_msg[me] = jnp.zeros(sel_msg.shape[1:], BF16)
-    sel_width = sel_msg.shape[2] - LANES
-    sel_msg[me, :, sel_width:] = pieces.astype(BF16)
+    selected = wsel.shape[0]
+    padded = sel_msg.shape[2]
+    lane = lax.broadcasted_iota(jnp.int32, (samples, padded), 1) - selected
+    pieces[...] = jnp.where(
+        lane == 0, high, jnp.where(lane == 1, low, jnp.where(lane == 2, rest, 0.0))
+    )
+    v_wsel[selected:, :] = jnp.zeros((padded - selected, channels), BF16)
 
     loads["again"].wait()
     for d in range(1, n):
@@ -188,12 +194,10 @@
         fresh = dot(normed[...], v_wkv[i]).astype(BF16)
         for g in range(groups):
             one = fresh[:, g * head_size : (g + 1) * head_size]
-            for s in range(share):
-                h = g * share + s
-                kv2[i, :, h * head_size : (h + 1) * head_size] = one
             wide = one.astype(F32)
             for s in range(8):
                 kv3[i, g, :, s, :] = wide
+            kv2[i, :, g * share : (g + 1) * share, :] = kv3[i, g].astype(BF16)[:, :share, :]
     pltpu.make_async_copy(kv2, nkv_out, out_sem.at[0]).start()
     q3[...] = jnp.zeros_like(q3)
     for g in range(groups):
@@ -246,10 +250,10 @@
     loads["wsel"].wait()
     base = jnp.broadcast_to(v_fb[...], (samples, channels))
     for k in range(taps - 1):
-        base = base + v_fs[:, k, :] * v_fw[k : k + 1, :]
+        base = base + v_fs[k] * v_fw[k : k + 1, :]
     conv[...] = base
     for k in range(taps - 2):
-        nfs[:, k, :] = v_fs[:, k + 1, :]
+        nfs[k] = v_fs[k + 1]
     for d in range(1, n):
         arrived(2, lambda s: mixfull.at[s], d)
     norm_blocks(mixfull, v_mgain, normed, width)
@@ -259,11 +263,13 @@
     conv_sum = conv[...] + x_inner * v_fw[taps - 1 : taps, :]
     conv_b = (conv_sum * jax.nn.sigmoid(conv_sum)).astype(BF16)
     conv[...] = conv_b.astype(F32)
-    sel_msg[me, :, :rank] = dot(conv_b, v_wsel[:, :rank]).astype(BF16)
-    sel_msg[me, :, rank : rank + 2 * states] = dot(conv_b, v_wsel[:, rank:]).astype(BF16)
+    picked = lax.dot_general(
+        conv_b, v_wsel[...], (((1,), (1,)), ((), ())), preferred_element_type=F32
+    )
+    sel_msg[me] = (picked + pieces[...]).astype(BF16)
     for d in range(1, n):
         send(3, sel_msg.at[me], sel_msg.at[me], d)
-    nfs[:, taps - 2, :] = x_inner
+    nfs[taps - 2] = x_inner
     pltpu.make_async_copy(nfs, nfs_out, out_sem.at[1]).start()
     loads["win1"].wait()
     matmul(normed, v_win.at[1], gate)
@@ -285,10 +291,8 @@
     bct[:samples, :] = projected[:, rank : rank + LANES]
     flipped = jnp.transpose(bct[...])
     bct[...] = flipped
-    total = jnp.sum(projected[:, sel_width:], axis=1, keepdims=True)
-    diagonal = lax.broadcasted_iota(jnp.int32, (samples, LANES), 0) == lane
-    row = jnp.sum(jnp.where(diagonal, total, 0.0), axis=0, keepdims=True)
-    rew[...] = row[:, :samples]
+    total = jnp.sum(jnp.where((lane >= 0) & (lane < 3), projected, 0.0), axis=1, keepdims=True)
+    rew[...] = jnp.sum(jnp.where(diagonal, total, 0.0), axis=0, keepdims=True)
 
     for b in range(samples):
         now = step[b : b + 1, :]
@@ -318,6 +322,47 @@
         ((kv2, nkv_out), (nfs, nfs_out), (v_scan, scan_out), (rew, rew_out), (hout, hidden_out))
     ):
         pltpu.make_async_copy(src, dst, out_sem.at[i]).wait()
+
+
+def hand_out_kernel(parts, *refs):
+    count = len(parts)
+    sources, targets = refs[:count], refs[count : 2 * count]
+    held = refs[2 * count : 3 * count]
+    in_sem, out_sem = refs[3 * count :]
+    pieces = []
+    for i, cuts in enumerate(parts):
+        rows = sources[i].shape[0] // cuts
+        for c in range(cuts):
+            pieces.append((i, pl.ds(c * rows, rows)))
+    copies = []
+    for k, (i, part) in enumerate(pieces):
+        arrive = pltpu.make_async_copy(sources[i].at[part], held[i].at[part], in_sem.at[k])
+        leave = pltpu.make_async_copy(held[i].at[part], targets[i].at[part], out_sem.at[k])
+        arrive.start()
+        copies.append((arrive, leave))
+    for arrive, leave in copies:
+        arrive.wait()
+        leave.start()
+    for arrive, leave in copies:
+        leave.wait()
+
+
+def hand_out(results):
+    parts = [1] * len(results)
+    for cuts in (8, 4, 2):
+        if results[3].shape[0] % cuts == 0:
+            parts[3] = cuts
+            break
+    total = sum(parts)
+    return pl.pallas_call(
+        functools.partial(hand_out_kernel, parts),
+        out_shape=tuple(jax.ShapeDtypeStruct(a.shape, a.dtype) for a in results),
+        in_specs=[pl.BlockSpec(memory_space=pl.ANY)] * len(results),
+        out_specs=[pl.BlockSpec(memory_space=pl.ANY)] * len(results),
+        scratch_shapes=[pltpu.VMEM(a.shape, a.dtype) for a in results]
+        + [pltpu.SemaphoreType.DMA((total,)), pltpu.SemaphoreType.DMA((total,))],
+        name="hand_out",
+    )(*results)
 
 
 def local(n, *args):
@@ -333,10 +378,11 @@
     states, channels = lrate.shape
     row = lambda a: a.reshape(1, a.shape[0])
     args = (
-        hidden, row(again), wq, wkv, wao, cache, lengths, row(mgain), w_in, fw, row(fb), fs,
-        wsel, wstep, row(sbias), lrate, row(skip), scan, wmo, rterm, rmask,
-    )
-    sel_pad = -(-wsel.shape[1] // LANES) * LANES + LANES
+        hidden, row(again), wq, wkv, wao, cache, lengths, row(mgain), w_in, fw, row(fb),
+        jnp.transpose(fs, (1, 0, 2)), wsel.T, wstep, row(sbias), lrate, row(skip), scan, wmo,
+        rterm.T, rmask.T,
+    )
+    sel_pad = -(-(wsel.shape[1] + 3) // LANES) * LANES
     same = lambda a: pltpu.VMEM(a.shape, a.dtype)
     scratch = [
         pltpu.VMEM((n, samples, width), BF16),
@@ -349,28 +395,28 @@
         same(w_in),
         same(fw),
         same(args[10]),
-        same(fs),
-        same(wsel),
+        same(args[11]),
+        pltpu.VMEM((sel_pad, channels), BF16),
         same(wstep),
         same(args[14]),
         same(lrate),
         same(args[16]),
         same(scan),
         same(wmo),
-        same(rterm),
-        same(rmask),
+        same(args[19]),
+        same(args[20]),
         pltpu.VMEM((samples, model), BF16),
         pltpu.VMEM((groups, samples, 8, head_size), F32),
         pltpu.VMEM((2, groups, samples, 8, head_size), F32),
         pltpu.VMEM((samples, 8, LANES), jnp.int32),
         pltpu.VMEM((samples, heads * head_size), F32),
-        pltpu.VMEM((2, samples, heads * head_size), BF16),
+        pltpu.VMEM((2, samples, heads, head_size), BF16),
         pltpu.VMEM((n, samples, width), BF16),
         pltpu.VMEM((n, samples, width), BF16),
         pltpu.VMEM((n, samples, width), BF16),
         pltpu.VMEM((samples, channels), F32),
         pltpu.VMEM((samples, channels), F32),
-        same(fs),
+        same(args[11]),
         pltpu.VMEM((n, samples, sel_pad), BF16),
         pltpu.VMEM((samples, channels), F32),
         pltpu.VMEM((samples, channels), F32),
@@ -381,6 +427,7 @@
         pltpu.VMEM((samples, width), BF16),
         pltpu.VMEM((LANES, LANES), F32),
         pltpu.VMEM((1, samples), F32),
+        pltpu.VMEM((samples, sel_pad), F32),
         pltpu.SemaphoreType.DMA((19 + 4 * groups,)),
         pltpu.SemaphoreType.DMA((5,)),
         pltpu.SemaphoreType.DMA((5, n)),
@@ -388,12 +435,12 @@
     ]
     in_specs = [pl.BlockSpec(memory_space=pl.ANY)] * len(args)
     in_specs[6] = pl.BlockSpec(memory_space=pltpu.SMEM)
-    hidden_out, nkv, nfs, new_scan, rewards = pl.pallas_call(
+    results = pl.pallas_call(
         functools.partial(kernel, n),
         out_shape=(
             jax.ShapeDtypeStruct((samples, width), BF16),
-            jax.ShapeDtypeStruct((2, samples, heads * head_size), BF16),
-            jax.ShapeDtypeStruct(fs.shape, F32),
+            jax.ShapeDtypeStruct((2, samples, heads, head_size), BF16),
+            jax.ShapeDtypeStruct(args[11].shape, F32),
             jax.ShapeDtypeStruct(scan.shape, F32),
             jax.ShapeDtypeStruct((1, samples), F32),
         ),
@@ -405,13 +452,8 @@
         ),
         name="decode_step",
     )(*args)
-    return (
-        hidden_out,
-        nkv.reshape(2, samples, heads, head_size),
-        nfs,
-        new_scan,
-        rewards.reshape(samples),
-    )
+    hidden_out, nkv, nfs, new_scan, rewards = hand_out(results)
+    return hidden_out, nkv, jnp.transpose(nfs, (1, 0, 2)), new_scan, rewards.reshape(samples)
 
 
 def solution(mesh):

time: 58 us -> 44.4 us (0.77)
  local copies, waits for them, and re-layouts: 15.4 us -> 0 us
  Pallas kernels: 41.5 us -> 43.6 us
    unnamed x8 -> x0, local copies, waits for them, and re-layouts: 14 us -> none
    pallas_call x0 -> x1, Pallas kernels: none -> 2.45 us  [hand_out(): pl.pallas_call(functools.partial(hand_out_kernel, parts), out_shape=tuple...]
    reshape x1 -> x0, local copies, waits for them, and re-layouts: 1.44 us -> none  [local(): nkv.reshape(2, samples, heads, head_size)]
where the time goes in v2:
time: 44.4 us; the launch traced here: 44.2 us
  Pallas kernels  43.6 us (98%)
  between operations  0.65 us (1%)
    pallas_call x1, Pallas kernels, local(): pl.pallas_call(functools.partial(kernel, n), out_shape=(jax.ShapeDtypeStr...  41.1 us
    pallas_call x1, Pallas kernels, hand_out(): pl.pallas_call(functools.partial(hand_out_kernel, parts), out_shape=tuple...  2.45 us

profile of v2, /device:TPU:0, one launch (start us, length us, event | category | flops | bytes accessed | tf_op | source)
XLA Modules:
  0.0 44.2 jit_solution(7842233643573759921)
XLA Ops:
  0.6 41.1 %decode_step.1 = (bf16[24,512]{1,0:T(8,128)(2,1)}, bf16[2,24,4,128]{3,2,1,0:T(4,128)(2,1)}, f32[3,24,1024]{2,1,0:T(8,128)}, f32[24,16,1024]{2,1,0:T(8,128)}, f32[1,24]{1,0:T(1,128)}) custom-call(bf16[24,512]{1,0:T(8,128)(2,1)} %refs_0_.1, f32[1,4096]{1,0:T(1,128)} %bitcast.13, bf16[4096,512]{1,0:T(8,128)(2,1)} %refs_2_.1, bf16[2,4096,512]{2,1,0:T(8,128)(2,1)} %refs_3_.1, ...), custom_call_target="tpu_custom_call" | custom-call | tf_op jit(solution)/shard_map/decode_step/pallas_call | solution.py:438
  41.8 2.4 %hand_out.1 = (bf16[24,512]{1,0:T(8,128)(2,1)}, bf16[2,24,4,128]{3,2,1,0:T(4,128)(2,1)}, f32[3,24,1024]{2,1,0:T(8,128)}, f32[24,16,1024]{2,1,0:T(8,128)}, f32[1,24]{1,0:T(1,128)}) custom-call(bf16[24,512]{1,0:T(8,128)(2,1)} %get-tuple-element.15.refs_0_, bf16[2,24,4,128]{3,2,1,0:T(4,128)(2,1)} %get-tuple-element.16.refs_1_, ...), custom_call_target="tpu_custom_call" | custom-call | tf_op jit(solution)/shard_map/hand_out/pallas_call | solution.py:357
